TPU v7x, 32 devices: a whole 2x2x4 slice. The times are simulated.
32 devices in a mesh: dp: 8 (over y, x, core), sub: 4 (over z).
Axes of the slice: x: 2, y: 2, z: 4, core: 2. Of those that a mesh axis runs over, the one named last changes fastest.
Arguments:
- queries: float32 [2048, 1024], P(('dp', 'sub')), may hold values from -8 to 8
- passages: float32 [2048, 1024], P(('dp', 'sub')), may hold values from -8 to 8
- positives: int32 [2048], P(('dp', 'sub')), may hold values from 0 to 2047, each once
Outputs:
- losses: float32 [2048], P(('dp', 'sub'))
- query_grads: float32 [2048, 1024], P(('dp', 'sub'))
- passage_grads: float32 [2048, 1024], P(('dp', 'sub'))
All inputs are finite; a program needn't handle non-finite values.
Results may differ from a plain program's by a relative error of at most 0.00185.
The roundings to bfloat16 on the way count: a program that leaves them out, or rounds other values in their place, can miss the bound.
Values may be sent and summed in bfloat16 or wider, within the bound.
A program may use at most 128 MiB of HBM per device.

v0:
```python
import jax
import jax.numpy as jnp
from jax import lax
from jax.sharding import PartitionSpec as P

logit_scale = 20.0


def row_scores(query_rows, passage_rows):
    return (
        lax.dot_general(
            query_rows, passage_rows, (((1,), (1,)), ((), ())), preferred_element_type=jnp.float32
        )
        * logit_scale
    )


def local_stats(scores, onehot):
    highest = jnp.max(scores, axis=1)
    exp_total = jnp.sum(jnp.exp(scores - highest[:, None]), axis=1)
    positive_score = jnp.sum(onehot * scores, axis=1)
    return (highest, exp_total, positive_score)


def body(queries, passages, positives):
    row_count = queries.shape[0]
    groups = lax.axis_size("sub")
    member = lax.axis_index("sub")
    query_half = queries.astype(jnp.bfloat16)
    passage_half = passages.astype(jnp.bfloat16)
    query_rows, row_targets = (
        lax.all_gather(query_half, "sub", axis=0, tiled=True),
        lax.all_gather(positives, "sub", axis=0, tiled=True),
    )
    width_cols = row_count * lax.axis_size("dp")
    passage_rows = lax.all_gather(passage_half, "dp", axis=0, tiled=True)
    scores = row_scores(query_rows, passage_rows)
    column = jnp.arange(width_cols, dtype=jnp.int32)
    column_ids = (column // row_count * groups + member) * row_count + column % row_count
    onehot = (column_ids[None, :] == row_targets[:, None]).astype(jnp.float32)
    highest, exp_total, positive_score = local_stats(scores, onehot)
    overall = lax.pmax(highest, "sub")
    exp_total, positive_score = lax.psum(
        (exp_total * jnp.exp(highest - overall), positive_score), "sub"
    )
    highest = overall
    log_norm = highest + jnp.log(exp_total)
    losses = lax.dynamic_slice_in_dim(log_norm - positive_score, member * row_count, row_count)
    weights = ((jnp.exp(scores - log_norm[:, None]) - onehot) * logit_scale).astype(jnp.bfloat16)
    query_terms = jnp.dot(weights, passage_rows, preferred_element_type=jnp.float32)
    query_grads = lax.psum_scatter(query_terms, "sub", scatter_dimension=0, tiled=True)
    passage_grads = lax.psum_scatter(
        lax.dot_general(
            weights, query_rows, (((0,), (0,)), ((), ())), preferred_element_type=jnp.float32
        ),
        "dp",
        scatter_dimension=0,
        tiled=True,
    )
    return (losses, query_grads, passage_grads)


def solution(mesh):
    placed = (P(("dp", "sub"), None), P(("dp", "sub"), None), P(("dp", "sub")))
    return jax.shard_map(
        body,
        mesh=mesh,
        in_specs=placed,
        out_specs=(P(("dp", "sub")), P(("dp", "sub"), None), P(("dp", "sub"), None)),
        check_vma=False,
    )
```

profile of v0, /device:TPU:0, one launch (start us, length us, event | category | flops | bytes accessed | tf_op | source)
XLA Modules:
  0.0 138.0 jit_solution(5630810498335591611)
XLA Ops:
  7.2 0.0 all-gather.2.cloned.1.call-start
  7.2 1.6 %convert_element_type.13 = bf16[64,1024]{1,0:T(8,128)(2,1)} convert(f32[64,1024]{1,0:T(8,128)} %param.4) | non-fusion elementwise | flops 65536 | bytes 393216 | tf_op jit(solution)/shard_map/convert_element_type | solution.py:30
  8.8 0.0 all-gather.2.cloned.1.call-update
  8.9 0.0 reduce-scatter.3.cloned.1.call-start
  8.9 1.0 convert_element_type.12
  9.9 1.2 dynamic-slice
  11.8 0.9 dynamic-update-slice
  12.6 9.9 %all-reduce = s32[256]{0:T(256)S(1)} all-reduce(s32[256]{0:T(256)S(1)} %dynamic-update-slice), channel_id=1, replica_groups=mesh['dp'=8,'sub'=4] {'sub'}, use_global_device_ids=true, to_apply=%add | all-reduce | flops 256 | bytes 2048
  22.6 15.5 %all_gather.9 = bf16[256,1024]{1,0:T(8,128)(2,1)S(1)} all-gather(bf16[64,1024]{1,0:T(8,128)(2,1)S(1)} %convert_element_type.12), channel_id=1, replica_groups=mesh['dp'=8,'sub'=4] {'sub'}, dimensions={0}, use_global_device_ids=true | all-gather | bytes 655360 | tf_op jit(solution)/shard_map/all_gather | solution.py:32
  38.1 0.0 all-gather.2.cloned.1.call-done
  38.1 0.0 copy-start
  38.1 1.9 %fusion.20 = (f32[256]{0:T(256)S(1)}, f32[256,512]{1,0:T(8,128)S(1)}) fusion(bf16[256,1024]{1,0:T(8,128)(2,1)S(1)} %all_gather.9, bf16[512,1024]{1,0:T(8,128)(2,1)} %all-gather.2.cloned.1.call-done), kind=kOutput, calls=%fused_computation.28 | convolution fusion | flops 268697344 | bytes 2098176 | tf_op jit(solution)/shard_map/dot_general | solution.py:11
  40.0 10.7 %pmax.7 = f32[256]{0:T(256)S(1)} all-reduce(f32[256]{0:T(256)S(1)} %get-tuple-element.9), channel_id=1, replica_groups=mesh['dp'=8,'sub'=4] {'sub'}, use_global_device_ids=true, to_apply=%region_1.2 | all-reduce | flops 256 | bytes 2048 | tf_op jit(solution)/shard_map/pmax | solution.py:42
  50.7 0.3 fusion
  51.0 8.4 %all-reduce.1 = (f32[256]{0:T(256)S(1)}, f32[256]{0:T(256)S(1)}) all-reduce(f32[256]{0:T(256)S(1)} %exponential_multiply_fusion, f32[256]{0:T(256)S(1)} %get-tuple-element.3), channel_id=1, replica_groups=mesh['dp'=8,'sub'=4] {'sub'}, use_global_device_ids=true, to_apply=%region_3.4 | all-reduce | flops 512 | bytes 4096 | tf_op jit(solution)/shard_map/psum | solution.py:43
  59.3 0.0 copy-done
  59.3 1.5 %fusion.17 = f32[256,1024]{1,0:T(8,128)} fusion(bf16[512,1024]{1,0:T(8,128)(2,1)S(1)} %copy-done, f32[256,512]{1,0:T(8,128)S(1)} %get-tuple-element.10, f32[256]{0:T(256)S(1)} %get-tuple-element.8, s32[512]{0:T(512)S(1)} %fusion.11, s32[256]{0:T(256)S(1)} %all-reduce), kind=kOutput, calls=%fused_computation.26 | convolution fusion | flops 269221888 | bytes 2625536 | tf_op jit(solution)/shard_map/dot_general | solution.py:50
  60.9 0.0 reduce-scatter.3.cloned.1.call-update
  60.9 0.0 reduce-scatter.5.cloned.1.call-start
  60.9 2.0 %fusion.15 = f32[512,1024]{1,0:T(8,128)} fusion(bf16[256,1024]{1,0:T(8,128)(2,1)S(1)} %all_gather.9, f32[256,512]{1,0:T(8,128)S(1)} %get-tuple-element.10, f32[256]{0:T(256)S(1)} %get-tuple-element.8, s32[512]{0:T(512)S(1)} %fusion.11, s32[256]{0:T(256)S(1)} %all-reduce), kind=kOutput, calls=%fused_computation.25 | convolution fusion | flops 269221888 | bytes 3149824 | tf_op jit(solution)/shard_map/dot_general | solution.py:53
  62.9 0.0 reduce-scatter.5.cloned.1.call-update
  62.9 0.6 dynamic_slice.3
  63.5 24.4 %reduce-scatter.3.cloned.1.call-done = f32[64,1024]{1,0:T(8,128)} async-done(((f32[256,1024]{1,0:T(8,128)}), f32[64,1024]{1,0:T(8,128)}) %reduce-scatter.3.cloned.1.call-update) | async-done | bytes 262160 | tf_op jit(solution)/shard_map/reduce_scatter | solution.py:51
  88.0 43.5 %reduce-scatter.5.cloned.1.call-done = f32[64,1024]{1,0:T(8,128)} async-done(((f32[512,1024]{1,0:T(8,128)}), f32[64,1024]{1,0:T(8,128)}) %reduce-scatter.5.cloned.1.call-update) | async-done | bytes 262160 | tf_op jit(solution)/shard_map/reduce_scatter | solution.py:52
  (4 shorter events, 0.0 us)
Async XLA Ops:
  7.2 30.9 %all-gather.2.cloned.1.call-start = ((), (), s32[]{:S(2)}) async-start(), calls=%async_computation.2 | async-start | bytes 1179648 | tf_op jit(solution)/shard_map/all_gather | solution.py:36
  8.9 79.1 %reduce-scatter.3.cloned.1.call-start = ((), (), s32[]{:S(2)}) async-start(), calls=%async_computation.3 | async-start | bytes 1310720 | tf_op jit(solution)/shard_map/reduce_scatter | solution.py:51
  38.1 21.3 %copy-start = (bf16[512,1024]{1,0:T(8,128)(2,1)S(1)}, bf16[512,1024]{1,0:T(8,128)(2,1)}, u32[]{:S(2)}) copy-start(bf16[512,1024]{1,0:T(8,128)(2,1)} %all-gather.2.cloned.1.call-done) | copy-start | bytes 3145732
  60.9 70.6 %reduce-scatter.5.cloned.1.call-start = ((), (), s32[]{:S(2)}) async-start(), calls=%async_computation.4 | async-start | bytes 2359296 | tf_op jit(solution)/shard_map/reduce_scatter | solution.py:52
Sparse Core Ops, SparseCore 0:
  10.4 26.0 all-gather.1
  61.0 26.9 reduce-scatter.2
  91.8 39.5 reduce-scatter.4
where the time goes:
time: 138 us
  waiting for transfers between devices  68 us (49%)
  blocking collectives  44.5 us (32%)
  between operations  14.4 us (10%)
  matrix products  5.35 us (4%)
  other arithmetic  2.9 us (2%)
  local copies, waits for them, and re-layouts  2.69 us (2%)
    reduce_scatter x1, waiting for transfers between devices, body(): lax.psum_scatter(lax.dot_general(weights, query_rows, (((0,), (0,)), ((),...  43.5 us
    reduce_scatter x1, waiting for transfers between devices, body(): lax.psum_scatter(query_terms, 'sub', scatter_dimension=0, tiled=True)  24.4 us
    all_gather x1, blocking collectives, body(): lax.all_gather(query_half, 'sub', axis=0, tiled=True)  15.5 us
    pmax x1, blocking collectives, body(): overall = lax.pmax(highest, 'sub')  10.7 us
    unnamed x1, blocking collectives  9.92 us
    psum x1, blocking collectives, body(): lax.psum((exp_total * jnp.exp(highest - overall), positive_score), 'sub')  8.37 us
  transfers between devices with their start and end apart: 3, of which 2 were waited for; matrix products, arithmetic and copies ran while one was open for 4% of the time, Pallas kernels for 0%

commit v1 on v0

v1 whole, which is shorter than its diff:
```python
import functools

import jax
import jax.numpy as jnp
from jax import lax
from jax.experimental import pallas as pl
from jax.experimental.pallas import tpu as pltpu
from jax.sharding import PartitionSpec as P

logit_scale = 20.0
MESH = pl.DeviceIdType.MESH
CHUNKS = 2


class Copies:
    def __init__(self, send_sems, recv_sems, some_device):
        self.send_sems, self.recv_sems, self.some_device = send_sems, recv_sems, some_device
        self.sent, self.numbers = [], {}

    def number(self, key):
        return self.numbers.setdefault(key, len(self.numbers))

    def send(self, key, src, dst, device):
        i = self.number(key)
        copy = pltpu.make_async_remote_copy(
            src_ref=src, dst_ref=dst, send_sem=self.send_sems.at[i], recv_sem=self.recv_sems.at[i],
            device_id=device, device_id_type=MESH)
        copy.start()
        self.sent.append(copy)

    def arrive(self, key, dst):
        i = self.number(key)
        pltpu.make_async_remote_copy(
            src_ref=dst, dst_ref=dst, send_sem=self.send_sems.at[i], recv_sem=self.recv_sems.at[i],
            device_id=self.some_device, device_id_type=MESH).wait_recv()

    def finish(self):
        for copy in self.sent:
            copy.wait_send()


def kernel(nd, ns, q_ref, p_ref, t_ref, loss_ref, qg_ref, pg_ref,
           qall, pall, tall, st, wt, w, stat_out, stat_in, qpart, qsend, qrecv,
           ppart, ppartner, psend, precv, send_sems, recv_sems):
    rows, width = q_ref.shape
    nh, nz = nd // 4, ns // 2
    chips = nh * nz
    dp, sub = lax.axis_index("dp"), lax.axis_index("sub")
    core, x, h = dp % 2, (dp // 2) % 2, dp // 4
    l, s = sub % 2, sub // 2

    def device(dx=0, dl=0, dh=0, ds=0, dc=0):
        there = ((h + dh) % nh) * 4 + ((x + dx) % 2) * 2 + (core + dc) % 2
        return (there, ((s + ds) % nz) * 2 + (l + dl) % 2)

    partner = device(dc=1)
    peers = [device(dx=a // 2, dl=a % 2) for a in range(1, 4)]
    peers += [device(dh=b % nh, ds=b // nh) for b in range(1, chips)] + [partner]
    barrier = pltpu.get_barrier_semaphore()
    for peer in peers:
        pl.semaphore_signal(barrier, inc=1, device_id=peer, device_id_type=MESH)
    qall[pl.ds(0, rows), :] = q_ref[...].astype(jnp.bfloat16)
    pall[pl.ds(0, rows), :] = p_ref[...].astype(jnp.bfloat16)
    tall[0] = t_ref[...]
    pl.semaphore_wait(barrier, len(peers))

    copies = Copies(send_sems, recv_sems, partner)
    piece = rows // CHUNKS

    def block(ref, slot, part=None):
        if part is None:
            return ref.at[pl.ds(slot * rows, rows), :]
        return ref.at[pl.ds(slot * rows + part * piece, piece), :]

    def pslot(dc, ds, dh):
        return (dc * nz + ds % nz) * nh + dh % nh

    def to_partner(ds, dh, part=None):
        copies.send(("pc", ds, dh, part), block(pall, pslot(0, ds, dh), part),
                    block(pall, pslot(1, ds, dh), part), partner)

    for part in range(CHUNKS):
        copies.send(("ql", part), block(qall, 0, part), block(qall, 1, part), device(dl=1))
    for ds in range(1, nz):
        for part in range(CHUNKS):
            copies.send(("ps", (-ds) % nz, part), block(pall, 0, part),
                        block(pall, pslot(0, -ds, 0), part), device(ds=ds))
    copies.send(("qx",), block(qall, 0), block(qall, 2), device(dx=1))
    for dh in range(1, nh):
        copies.send(("ph", (-dh) % nh), block(pall, 0), block(pall, pslot(0, 0, -dh)), device(dh=dh))
    to_partner(0, 0)
    for a in range(1, 4):
        copies.send(("t", a), tall.at[0], tall.at[a], device(dx=a // 2, dl=a % 2))

    for part in range(CHUNKS):
        copies.arrive(("ql", part), block(qall, 1, part))
        copies.send(("qd", part), block(qall, 1, part), block(qall, 3, part), device(dx=1))
    for dh in range(1, nh):
        copies.arrive(("ph", dh), block(pall, pslot(0, 0, dh)))
        to_partner(0, dh)
    for part in range(CHUNKS):
        for ds in range(1, nz):
            here = block(pall, pslot(0, ds, 0), part)
            copies.arrive(("ps", ds, part), here)
            for dh in range(1, nh):
                copies.send(("pd", ds, (-dh) % nh, part), here,
                            block(pall, pslot(0, ds, -dh), part), device(dh=dh))
            to_partner(ds, 0, part)
    copies.arrive(("qx",), block(qall, 2))
    for part in range(CHUNKS):
        copies.arrive(("qd", part), block(qall, 3, part))
    for a in range(1, 4):
        copies.arrive(("t", a), tall.at[a])

    targets = jnp.concatenate([tall[a] for a in range(4)], axis=1)
    queries = 4 * rows
    span = nh * rows
    stats = None

    def onehot_of(dc, ds):
        lines = lax.broadcasted_iota(jnp.int32, (rows, queries), 0)
        parts = []
        for dh in range(nh):
            there, along = device(dh=dh, ds=ds, dc=dc)
            parts.append(lines + (there * ns + along) * rows == targets)
        return parts

    def score(dc, ds, stats):
        base = (dc * nz + ds) * span
        for dh in range(0, nh, 2):
            count = min(2, nh - dh) * rows
            at = pl.ds(base + dh * rows, count)
            st[at, :] = logit_scale * lax.dot_general(
                pall[at, :], qall[...], (((1,), (1,)), ((), ())), preferred_element_type=jnp.float32)
        tile = st[pl.ds(base, span), :]
        top = jnp.max(tile, axis=0, keepdims=True)
        positive = jnp.zeros((1, queries), jnp.float32)
        for dh, hit in enumerate(onehot_of(dc, ds)):
            positive += jnp.sum(jnp.where(hit, tile[dh * rows:(dh + 1) * rows], 0.0), axis=0, keepdims=True)
        if stats is not None:
            top = jnp.maximum(top, stats[0])
        total = jnp.sum(jnp.exp(tile - top), axis=0, keepdims=True)
        if stats is not None:
            total += stats[1] * jnp.exp(stats[0] - top)
            positive += stats[2]
        return top, total, positive

    stats = score(0, 0, stats)
    for dh in range(nh):
        copies.arrive(("pc", 0, dh, None), block(pall, pslot(1, 0, dh)))
    stats = score(1, 0, stats)
    for ds in range(1, nz):
        for dh in range(1, nh):
            for part in range(CHUNKS):
                copies.arrive(("pd", ds, dh, part), block(pall, pslot(0, ds, dh), part))
            to_partner(ds, dh)
        stats = score(0, ds, stats)
        for part in range(CHUNKS):
            copies.arrive(("pc", ds, 0, part), block(pall, pslot(1, ds, 0), part))
        for dh in range(1, nh):
            copies.arrive(("pc", ds, dh, None), block(pall, pslot(1, ds, dh)))
        stats = score(1, ds, stats)

    stat_out[...] = jnp.concatenate(list(stats) + [jnp.zeros((5, queries), jnp.float32)], axis=0)
    for a in range(1, 4):
        copies.send(("s", a), stat_out, stat_in.at[a - 1], device(dx=a // 2, dl=a % 2))
    top, total, positive = stats
    for a in range(1, 4):
        copies.arrive(("s", a), stat_in.at[a - 1])
        theirs = stat_in[a - 1]
        halves = [theirs[:, :2 * rows], theirs[:, 2 * rows:]]
        if a // 2:
            halves.reverse()
        if a % 2:
            halves = [jnp.concatenate([v[:, rows:], v[:, :rows]], axis=1) for v in halves]
        theirs = jnp.concatenate(halves, axis=1)
        higher = jnp.maximum(top, theirs[0:1])
        total = total * jnp.exp(top - higher) + theirs[1:2] * jnp.exp(theirs[0:1] - higher)
        positive += theirs[2:3]
        top = higher
    log_norm = top + jnp.log(total)
    loss_ref[...] = (log_norm - positive)[:, :rows]

    for dc in range(2):
        for ds in range(nz):
            base = (dc * nz + ds) * span
            for dh, hit in enumerate(onehot_of(dc, ds)):
                at = pl.ds(base + dh * rows, rows)
                weights = (jnp.exp(st[at, :] - log_norm) - hit.astype(jnp.float32)) * logit_scale
                wt[at, :] = weights.astype(jnp.bfloat16)
    for i in range(2 * chips * rows // (2 * rows)):
        at = pl.ds(i * 2 * rows, 2 * rows)
        w[:, at] = wt[at, :].T

    step = 2 * rows
    half = chips * rows

    def passage_terms(first):
        for i in range(half // step):
            ppart[pl.ds(first + i * step, step), :] = jnp.dot(
                wt[pl.ds(first + i * step, step), :], qall[...], preferred_element_type=jnp.float32)

    passage_terms(half)
    copies.send(("pp",), ppart.at[pl.ds(half, half), :], ppartner, partner)
    for pair in (1, 0):
        at = pl.ds(pair * 2 * rows, 2 * rows)
        qpart[at, :] = jnp.dot(w[at, :], pall[...], preferred_element_type=jnp.float32)
        for a in (2 * pair + 1, 2 * pair):
            if a:
                qsend[a - 1] = qpart[pl.ds(a * rows, rows), :].astype(jnp.bfloat16)
                copies.send(("q", a), qsend.at[a - 1], qrecv.at[a - 1], device(dx=a // 2, dl=a % 2))
    passage_terms(0)
    copies.arrive(("pp",), ppartner)
    for ds in reversed(range(nz)):
        for dh in reversed(range(nh)):
            b = ds * nh + dh
            if b:
                at = pl.ds(b * rows, rows)
                psend[b - 1] = (ppart[at, :] + ppartner[at, :]).astype(jnp.bfloat16)
                back = ((-ds) % nz) * nh + (-dh) % nh
                copies.send(("p", back), psend.at[b - 1], precv.at[back - 1], device(dh=dh, ds=ds))
    grads = qpart[pl.ds(0, rows), :]
    for a in range(1, 4):
        copies.arrive(("q", a), qrecv.at[a - 1])
        grads += qrecv[a - 1].astype(jnp.float32)
    qg_ref[...] = grads
    grads = ppart[pl.ds(0, rows), :] + ppartner[pl.ds(0, rows), :]
    for b in range(1, chips):
        copies.arrive(("p", b), precv.at[b - 1])
        grads += precv[b - 1].astype(jnp.float32)
    pg_ref[...] = grads
    copies.finish()


def body(nd, ns, queries, passages, positives):
    rows, width = queries.shape
    nh, nz = nd // 4, ns // 2
    chips = nh * nz
    half, cols = chips * rows, 2 * chips * rows
    bf16, f32 = jnp.bfloat16, jnp.float32
    copies = 16 + 4 * CHUNKS + chips * (3 + 3 * CHUNKS)
    losses, query_grads, passage_grads = pl.pallas_call(
        functools.partial(kernel, nd, ns),
        out_shape=(
            jax.ShapeDtypeStruct((1, rows), f32),
            jax.ShapeDtypeStruct((rows, width), f32),
            jax.ShapeDtypeStruct((rows, width), f32),
        ),
        in_specs=[pl.BlockSpec(memory_space=pltpu.VMEM)] * 3,
        out_specs=(pl.BlockSpec(memory_space=pltpu.VMEM),) * 3,
        scratch_shapes=[
            pltpu.VMEM((4 * rows, width), bf16),
            pltpu.VMEM((cols, width), bf16),
            pltpu.VMEM((4, 1, rows), jnp.int32),
            pltpu.VMEM((cols, 4 * rows), f32),
            pltpu.VMEM((cols, 4 * rows), bf16),
            pltpu.VMEM((4 * rows, cols), bf16),
            pltpu.VMEM((8, 4 * rows), f32),
            pltpu.VMEM((3, 8, 4 * rows), f32),
            pltpu.VMEM((4 * rows, width), f32),
            pltpu.VMEM((3, rows, width), bf16),
            pltpu.VMEM((3, rows, width), bf16),
            pltpu.VMEM((cols, width), f32),
            pltpu.VMEM((half, width), f32),
            pltpu.VMEM((chips - 1, rows, width), bf16),
            pltpu.VMEM((chips - 1, rows, width), bf16),
            pltpu.SemaphoreType.DMA((copies,)),
            pltpu.SemaphoreType.DMA((copies,)),
        ],
        compiler_params=pltpu.CompilerParams(
            collective_id=0, has_side_effects=True, vmem_limit_bytes=64 * 1024 * 1024 - 65536
        ),
    )(queries, passages, positives.reshape(1, rows))
    return losses.reshape(rows), query_grads, passage_grads


def solution(mesh):
    placed = (P(("dp", "sub"), None), P(("dp", "sub"), None), P(("dp", "sub")))
    return jax.shard_map(
        functools.partial(body, mesh.shape["dp"], mesh.shape["sub"]),
        mesh=mesh,
        in_specs=placed,
        out_specs=(P(("dp", "sub")), P(("dp", "sub"), None), P(("dp", "sub"), None)),
        check_vma=False,
    )
```

time: 138 us -> 45.1 us (0.33)
  waiting for transfers between devices: 68 us -> 0 us
  blocking collectives: 44.5 us -> 0 us
  Pallas kernels: 0 us -> 40.7 us
  between operations: 14.4 us -> 0.65 us
  matrix products: 5.35 us -> 0 us
  other arithmetic: 2.9 us -> 0 us
    reduce_scatter x2 -> x0, waiting for transfers between devices: 68 us -> none  [the longest x1 43.5 us: body(): lax.psum_scatter(lax.dot_general(weights, query_rows, (((0,), (0,)), ((),...]
    pallas_call x0 -> x1, Pallas kernels: none -> 40.7 us  [body(): pl.pallas_call(functools.partial(kernel, nd, ns), out_shape=(jax.ShapeDty...]
    all_gather x1 -> x0, blocking collectives: 15.5 us -> none  [body(): lax.all_gather(query_half, 'sub', axis=0, tiled=True)]
    pmax x1 -> x0, blocking collectives: 10.7 us -> none  [body(): overall = lax.pmax(highest, 'sub')]
    unnamed x1 -> x0, blocking collectives: 9.92 us -> none
    psum x1 -> x0, blocking collectives: 8.37 us -> none  [body(): lax.psum((exp_total * jnp.exp(highest - overall), positive_score), 'sub')]
    dot_general x3 -> x0, matrix products: 5.35 us -> none  [the longest x1 1.97 us: body(): lax.dot_general(weights, query_rows, (((0,), (0,)), ((), ())), preferred_...]
    convert_element_type x2 -> x0, other arithmetic: 2.59 us -> none  [the longest x1 1.62 us: body(): passage_half = passages.astype(jnp.bfloat16)]
  transfers between devices with their start and end apart: 3 -> 0, of which waited for: 2 -> 0; matrix products, arithmetic and copies ran while one was open for 4% -> 0% of each run, Pallas kernels for 0% -> 0%
where the time goes in v1:
time: 45.1 us; the launch traced here: 44.9 us
  Pallas kernels  40.7 us (90%)
  local copies, waits for them, and re-layouts  3.56 us (8%)
  between operations  0.65 us (1%)
    pallas_call x1, Pallas kernels, body(): pl.pallas_call(functools.partial(kernel, nd, ns), out_shape=(jax.ShapeDty...  40.7 us
    unnamed x7, local copies, waits for them, and re-layouts  3.56 us

profile of v1, /device:TPU:0, one launch (start us, length us, event | category | flops | bytes accessed | tf_op | source)
XLA Modules:
  0.0 44.9 jit_solution(2462785446852336565)
XLA Ops:
  0.6 40.7 %shard_map.58 = (f32[1,64]{1,0:T(1,128)}, f32[64,1024]{1,0:T(8,128)}, f32[64,1024]{1,0:T(8,128)}) custom-call(f32[64,1024]{1,0:T(8,128)} %q_ref.1, f32[64,1024]{1,0:T(8,128)} %p_ref.1, s32[1,64]{1,0:T(1,128)} %bitcast.2), custom_call_target="tpu_custom_call" | custom-call | tf_op jit(solution)/shard_map/pallas_call | solution.py:242
  41.3 0.0 copy-start.1
  41.4 0.6 %copy-done.1 = f32[1,64]{1,0:T(1,128)S(1)} copy-done((f32[1,64]{1,0:T(1,128)S(1)}, f32[1,64]{1,0:T(1,128)}, u32[]{:S(2)}) %copy-start.1) | copy-done | bytes 280
  42.0 0.5 %copy.9 = f32[64]{0:T(128)} copy(f32[64]{0:T(128)S(1)} %bitcast.3) | data formatting | bytes 512
  42.5 0.0 copy-start
  42.5 1.7 %copy.10 = f32[64,1024]{1,0:T(8,128)} copy(f32[64,1024]{1,0:T(8,128)} %get-tuple-element.13) | data formatting | bytes 524288
  44.2 0.0 copy-done
  44.2 0.7 %copy.11 = f32[64,1024]{1,0:T(8,128)} copy(f32[64,1024]{1,0:T(8,128)S(1)} %copy-done) | data formatting | bytes 524288
Async XLA Ops:
  41.3 0.6 %copy-start.1 = (f32[1,64]{1,0:T(1,128)S(1)}, f32[1,64]{1,0:T(1,128)}, u32[]{:S(2)}) copy-start(f32[1,64]{1,0:T(1,128)} %get-tuple-element.6) | copy-start | bytes 772
  42.5 1.7 %copy-start = (f32[64,1024]{1,0:T(8,128)S(1)}, f32[64,1024]{1,0:T(8,128)}, u32[]{:S(2)}) copy-start(f32[64,1024]{1,0:T(8,128)} %get-tuple-element.14) | copy-start | bytes 786436

commit v2 on v1

--- a/solution.py
+++ b/solution.py
@@ -1,4 +1,5 @@
 import functools
+import math
 
 import jax
 import jax.numpy as jnp
@@ -9,7 +10,7 @@
 
 logit_scale = 20.0
 MESH = pl.DeviceIdType.MESH
-CHUNKS = 2
+CHUNKS = 4
 
 
 class Copies:
@@ -39,9 +40,9 @@
             copy.wait_send()
 
 
-def kernel(nd, ns, q_ref, p_ref, t_ref, loss_ref, qg_ref, pg_ref,
+def kernel(nd, ns, q_ref, p_ref, t_ref, out_ref,
            qall, pall, tall, st, wt, w, stat_out, stat_in, qpart, qsend, qrecv,
-           ppart, ppartner, psend, precv, send_sems, recv_sems):
+           ppart, ppartner, pmid, psend, precv, send_sems, recv_sems):
     rows, width = q_ref.shape
     nh, nz = nd // 4, ns // 2
     chips = nh * nz
@@ -54,8 +55,8 @@
         return (there, ((s + ds) % nz) * 2 + (l + dl) % 2)
 
     partner = device(dc=1)
-    peers = [device(dx=a // 2, dl=a % 2) for a in range(1, 4)]
-    peers += [device(dh=b % nh, ds=b // nh) for b in range(1, chips)] + [partner]
+    peers = [device(dx=1), device(dl=1), partner]
+    peers += [device(dh=dh) for dh in range(1, nh)] + [device(ds=ds) for ds in range(1, nz)]
     barrier = pltpu.get_barrier_semaphore()
     for peer in peers:
         pl.semaphore_signal(barrier, inc=1, device_id=peer, device_id_type=MESH)
@@ -89,12 +90,14 @@
     for dh in range(1, nh):
         copies.send(("ph", (-dh) % nh), block(pall, 0), block(pall, pslot(0, 0, -dh)), device(dh=dh))
     to_partner(0, 0)
-    for a in range(1, 4):
-        copies.send(("t", a), tall.at[0], tall.at[a], device(dx=a // 2, dl=a % 2))
+    copies.send(("t", 1), tall.at[0], tall.at[1], device(dl=1))
+    copies.send(("t", 2), tall.at[0], tall.at[2], device(dx=1))
 
     for part in range(CHUNKS):
         copies.arrive(("ql", part), block(qall, 1, part))
         copies.send(("qd", part), block(qall, 1, part), block(qall, 3, part), device(dx=1))
+    copies.arrive(("t", 1), tall.at[1])
+    copies.send(("t", 3), tall.at[1], tall.at[3], device(dx=1))
     for dh in range(1, nh):
         copies.arrive(("ph", dh), block(pall, pslot(0, 0, dh)))
         to_partner(0, dh)
@@ -109,7 +112,7 @@
     copies.arrive(("qx",), block(qall, 2))
     for part in range(CHUNKS):
         copies.arrive(("qd", part), block(qall, 3, part))
-    for a in range(1, 4):
+    for a in range(2, 4):
         copies.arrive(("t", a), tall.at[a])
 
     targets = jnp.concatenate([tall[a] for a in range(4)], axis=1)
@@ -179,7 +182,7 @@
         positive += theirs[2:3]
         top = higher
     log_norm = top + jnp.log(total)
-    loss_ref[...] = (log_norm - positive)[:, :rows]
+    out_ref[pl.ds(2 * rows, 1), pl.ds(0, rows)] = (log_norm - positive)[:, :rows]
 
     for dc in range(2):
         for ds in range(nz):
@@ -195,41 +198,87 @@
     step = 2 * rows
     half = chips * rows
 
-    def passage_terms(first):
-        for i in range(half // step):
-            ppart[pl.ds(first + i * step, step), :] = jnp.dot(
-                wt[pl.ds(first + i * step, step), :], qall[...], preferred_element_type=jnp.float32)
-
-    passage_terms(half)
-    copies.send(("pp",), ppart.at[pl.ds(half, half), :], ppartner, partner)
-    for pair in (1, 0):
+    def passage_terms(dc, ds):
+        first = dc * half + ds * span
+        for i in range(-(-span // step)):
+            at = pl.ds(first + i * step, min(step, span - i * step))
+            ppart[at, :] = jnp.dot(wt[at, :], qall[...], preferred_element_type=jnp.float32)
+        if dc:
+            for dh in reversed(range(nh)):
+                b = ds * nh + dh
+                copies.send(("pp", b), block(ppart, chips + b), block(ppartner, b), partner)
+
+    def both_cores(ds, dh):
+        b = ds * nh + dh
+        copies.arrive(("pp", b), block(ppartner, b))
+        at = pl.ds(b * rows, rows)
+        return at, ppart[at, :] + ppartner[at, :]
+
+    def query_terms(pair):
         at = pl.ds(pair * 2 * rows, 2 * rows)
         qpart[at, :] = jnp.dot(w[at, :], pall[...], preferred_element_type=jnp.float32)
         for a in (2 * pair + 1, 2 * pair):
             if a:
                 qsend[a - 1] = qpart[pl.ds(a * rows, rows), :].astype(jnp.bfloat16)
                 copies.send(("q", a), qsend.at[a - 1], qrecv.at[a - 1], device(dx=a // 2, dl=a % 2))
-    passage_terms(0)
-    copies.arrive(("pp",), ppartner)
-    for ds in reversed(range(nz)):
-        for dh in reversed(range(nh)):
-            b = ds * nh + dh
-            if b:
-                at = pl.ds(b * rows, rows)
-                psend[b - 1] = (ppart[at, :] + ppartner[at, :]).astype(jnp.bfloat16)
-                back = ((-ds) % nz) * nh + (-dh) % nh
-                copies.send(("p", back), psend.at[b - 1], precv.at[back - 1], device(dh=dh, ds=ds))
+
+    for ds in reversed(range(1, nz)):
+        passage_terms(1, ds)
+        passage_terms(0, ds)
+    query_terms(1)
+    for ds in reversed(range(1, nz)):
+        for dh in reversed(range(1, nh)):
+            at, both = both_cores(ds, dh)
+            ppart[at, :] = both
+            for part in range(CHUNKS):
+                here = ((ds - 1) * (nh - 1) + nh - dh - 1)
+                copies.send(("pm", ds, nh - dh, part), block(ppart, ds * nh + dh, part),
+                            block(pmid, here, part), device(dh=dh))
+    passage_terms(1, 0)
+    passage_terms(0, 0)
+    query_terms(0)
+    for dh in reversed(range(1, nh)):
+        at, both = both_cores(0, dh)
+        psend[pl.ds((dh - 1) * rows, rows), :] = both.astype(jnp.bfloat16)
+        copies.send(("p", nh - dh), block(psend, dh - 1), block(precv, nh - dh - 1), device(dh=dh))
+    for ds in range(1, nz):
+        at, both = both_cores(ds, 0)
+        ppart[at, :] = both
+        for part in range(CHUNKS):
+            total = ppart[pl.ds(ds * span + part * piece, piece), :]
+            for dh in range(1, nh):
+                here = (ds - 1) * (nh - 1) + dh - 1
+                copies.arrive(("pm", ds, dh, part), block(pmid, here, part))
+                total += pmid[pl.ds(here * rows + part * piece, piece), :]
+            slot = nh - 2 + ds
+            psend[pl.ds(slot * rows + part * piece, piece), :] = total.astype(jnp.bfloat16)
+            copies.send(("pz", nz - ds, part), block(psend, slot, part),
+                        block(precv, nh - 2 + nz - ds, part), device(ds=ds))
     grads = qpart[pl.ds(0, rows), :]
     for a in range(1, 4):
         copies.arrive(("q", a), qrecv.at[a - 1])
         grads += qrecv[a - 1].astype(jnp.float32)
-    qg_ref[...] = grads
-    grads = ppart[pl.ds(0, rows), :] + ppartner[pl.ds(0, rows), :]
-    for b in range(1, chips):
-        copies.arrive(("p", b), precv.at[b - 1])
-        grads += precv[b - 1].astype(jnp.float32)
-    pg_ref[...] = grads
+    out_ref[pl.ds(0, rows), :] = grads
+    at, grads = both_cores(0, 0)
+    for dh in range(1, nh):
+        copies.arrive(("p", dh), block(precv, dh - 1))
+        grads += precv[pl.ds((dh - 1) * rows, rows), :].astype(jnp.float32)
+    ppart[at, :] = grads
+    for part in range(CHUNKS):
+        grads = ppart[pl.ds(part * piece, piece), :]
+        for ds in range(1, nz):
+            copies.arrive(("pz", ds, part), block(precv, nh - 2 + ds, part))
+            at = pl.ds((nh - 2 + ds) * rows + part * piece, piece)
+            grads += precv[at, :].astype(jnp.float32)
+        out_ref[pl.ds(rows + part * piece, piece), :] = grads
     copies.finish()
+
+
+def unpack(packed_ref, loss_ref, qg_ref, pg_ref):
+    rows = qg_ref.shape[0]
+    loss_ref[...] = packed_ref[pl.ds(2 * rows, 1), pl.ds(0, rows)]
+    qg_ref[...] = packed_ref[pl.ds(0, rows), :]
+    pg_ref[...] = packed_ref[pl.ds(rows, rows), :]
 
 
 def body(nd, ns, queries, passages, positives):
@@ -238,39 +287,51 @@
     chips = nh * nz
     half, cols = chips * rows, 2 * chips * rows
     bf16, f32 = jnp.bfloat16, jnp.float32
-    copies = 16 + 4 * CHUNKS + chips * (3 + 3 * CHUNKS)
+    copies = 16 + 5 * CHUNKS + chips * (3 + 4 * CHUNKS)
+    scratch = [
+        ((4 * rows, width), bf16),
+        ((cols, width), bf16),
+        ((4, 1, rows), jnp.int32),
+        ((cols, 4 * rows), f32),
+        ((cols, 4 * rows), bf16),
+        ((4 * rows, cols), bf16),
+        ((8, 4 * rows), f32),
+        ((3, 8, 4 * rows), f32),
+        ((4 * rows, width), f32),
+        ((3, rows, width), bf16),
+        ((3, rows, width), bf16),
+        ((cols, width), f32),
+        ((half, width), f32),
+        ((max(1, (nz - 1) * (nh - 1)) * rows, width), f32),
+        ((max(1, nz + nh - 2) * rows, width), bf16),
+        ((max(1, nz + nh - 2) * rows, width), bf16),
+    ]
+    held = sum(math.prod(shape) * jnp.dtype(kind).itemsize for shape, kind in scratch)
+    vmem = pl.BlockSpec(memory_space=pltpu.VMEM)
+    packed = pl.pallas_call(
+        functools.partial(kernel, nd, ns),
+        out_shape=jax.ShapeDtypeStruct((2 * rows + 8, width), f32),
+        in_specs=[vmem] * 3,
+        out_specs=vmem,
+        scratch_shapes=[pltpu.VMEM(*entry) for entry in scratch] + [
+            pltpu.SemaphoreType.DMA((copies,)),
+            pltpu.SemaphoreType.DMA((copies,)),
+        ],
+        compiler_params=pltpu.CompilerParams(
+            collective_id=0, has_side_effects=True, vmem_limit_bytes=held + 8 * 1024 * 1024
+        ),
+    )(queries, passages, positives.reshape(1, rows))
     losses, query_grads, passage_grads = pl.pallas_call(
-        functools.partial(kernel, nd, ns),
+        unpack,
         out_shape=(
             jax.ShapeDtypeStruct((1, rows), f32),
             jax.ShapeDtypeStruct((rows, width), f32),
             jax.ShapeDtypeStruct((rows, width), f32),
         ),
-        in_specs=[pl.BlockSpec(memory_space=pltpu.VMEM)] * 3,
-        out_specs=(pl.BlockSpec(memory_space=pltpu.VMEM),) * 3,
-        scratch_shapes=[
-            pltpu.VMEM((4 * rows, width), bf16),
-            pltpu.VMEM((cols, width), bf16),
-            pltpu.VMEM((4, 1, rows), jnp.int32),
-            pltpu.VMEM((cols, 4 * rows), f32),
-            pltpu.VMEM((cols, 4 * rows), bf16),
-            pltpu.VMEM((4 * rows, cols), bf16),
-            pltpu.VMEM((8, 4 * rows), f32),
-            pltpu.VMEM((3, 8, 4 * rows), f32),
-            pltpu.VMEM((4 * rows, width), f32),
-            pltpu.VMEM((3, rows, width), bf16),
-            pltpu.VMEM((3, rows, width), bf16),
-            pltpu.VMEM((cols, width), f32),
-            pltpu.VMEM((half, width), f32),
-            pltpu.VMEM((chips - 1, rows, width), bf16),
-            pltpu.VMEM((chips - 1, rows, width), bf16),
-            pltpu.SemaphoreType.DMA((copies,)),
-            pltpu.SemaphoreType.DMA((copies,)),
-        ],
-        compiler_params=pltpu.CompilerParams(
-            collective_id=0, has_side_effects=True, vmem_limit_bytes=64 * 1024 * 1024 - 65536
-        ),
-    )(queries, passages, positives.reshape(1, rows))
+        in_specs=[vmem],
+        out_specs=(vmem,) * 3,
+        compiler_params=pltpu.CompilerParams(vmem_limit_bytes=8 * 1024 * 1024),
+    )(packed)
     return losses.reshape(rows), query_grads, passage_grads
 
 

time: 45.1 us -> 40.3 us (0.89)
  Pallas kernels: 40.7 us -> 36.9 us
  local copies, waits for them, and re-layouts: 3.56 us -> 2.55 us
    pallas_call x1 -> x2, Pallas kernels: 40.7 us -> 36.9 us  [the longest x1 36.1 us: body(): pl.pallas_call(functools.partial(kernel, nd, ns), out_shape=jax.ShapeDtyp...]
    unnamed x7 -> x6, local copies, waits for them, and re-layouts: 3.56 us -> 2.55 us
where the time goes in v2:
time: 40.3 us; the launch traced here: 40.1 us
  Pallas kernels  36.9 us (92%)
  local copies, waits for them, and re-layouts  2.55 us (6%)
  between operations  0.65 us (2%)
    pallas_call x1, Pallas kernels, body(): pl.pallas_call(functools.partial(kernel, nd, ns), out_shape=jax.ShapeDtyp...  36.1 us
    unnamed x6, local copies, waits for them, and re-layouts  2.55 us
    pallas_call x1, Pallas kernels, body(): pl.pallas_call(unpack, out_shape=(jax.ShapeDtypeStruct((1, rows), f32), j...  0.83 us

profile of v2, /device:TPU:0, one launch (start us, length us, event | category | flops | bytes accessed | tf_op | source)
XLA Modules:
  0.0 40.1 jit_solution(1773199007766768717)
XLA Ops:
  0.6 0.0 copy-start.2
  0.6 0.6 %copy-done.2 = s32[64]{0:T(128)S(1)} copy-done((s32[64]{0:T(128)S(1)}, s32[64]{0:T(128)}, u32[]{:S(2)}) %copy-start.2) | copy-done | bytes 280
  1.3 0.0 copy-start
  1.3 0.9 %copy-done = f32[64,1024]{1,0:T(8,128)S(1)} copy-done((f32[64,1024]{1,0:T(8,128)S(1)}, f32[64,1024]{1,0:T(8,128)}, u32[]{:S(2)}) %copy-start) | copy-done | bytes 262168
  2.2 0.0 copy-start.1
  2.2 0.9 %copy-done.1 = f32[64,1024]{1,0:T(8,128)S(1)} copy-done((f32[64,1024]{1,0:T(8,128)S(1)}, f32[64,1024]{1,0:T(8,128)}, u32[]{:S(2)}) %copy-start.1) | copy-done | bytes 262168
  3.2 36.1 %shard_map.58.packed_ref = f32[136,1024]{1,0:T(8,128)S(1)} custom-call(f32[64,1024]{1,0:T(8,128)S(1)} %copy-done, f32[64,1024]{1,0:T(8,128)S(1)} %copy-done.1, s32[1,64]{1,0:T(1,128)S(1)} %bitcast.2), custom_call_target="tpu_custom_call" | custom-call | tf_op jit(solution)/shard_map/pallas_call | solution.py:311
  39.3 0.8 %shard_map.59 = (f32[1,64]{1,0:T(1,128)}, f32[64,1024]{1,0:T(8,128)}, f32[64,1024]{1,0:T(8,128)}) custom-call(f32[136,1024]{1,0:T(8,128)S(1)} %shard_map.58.packed_ref), custom_call_target="tpu_custom_call" | custom-call | tf_op jit(solution)/shard_map/pallas_call | solution.py:324
Async XLA Ops:
  0.6 0.7 %copy-start.2 = (s32[64]{0:T(128)S(1)}, s32[64]{0:T(128)}, u32[]{:S(2)}) copy-start(s32[64]{0:T(128)} %param.5) | copy-start | bytes 772
  1.3 0.9 %copy-start = (f32[64,1024]{1,0:T(8,128)S(1)}, f32[64,1024]{1,0:T(8,128)}, u32[]{:S(2)}) copy-start(f32[64,1024]{1,0:T(8,128)} %q_ref.1) | copy-start | bytes 786436
  2.2 0.9 %copy-start.1 = (f32[64,1024]{1,0:T(8,128)S(1)}, f32[64,1024]{1,0:T(8,128)}, u32[]{:S(2)}) copy-start(f32[64,1024]{1,0:T(8,128)} %p_ref.1) | copy-start | bytes 786436

commit v3 on v2

--- a/solution.py
+++ b/solution.py
@@ -1,5 +1,4 @@
 import functools
-import math
 
 import jax
 import jax.numpy as jnp
@@ -10,7 +9,7 @@
 
 logit_scale = 20.0
 MESH = pl.DeviceIdType.MESH
-CHUNKS = 4
+CHUNKS = 2
 
 
 class Copies:
@@ -41,8 +40,8 @@
 
 
 def kernel(nd, ns, q_ref, p_ref, t_ref, out_ref,
-           qall, pall, tall, st, wt, w, stat_out, stat_in, qpart, qsend, qrecv,
-           ppart, ppartner, pmid, psend, precv, send_sems, recv_sems):
+           qin, pin, qall, pall, tall, st, wt, w, stat_out, stat_in, qpart, qsend, qrecv,
+           ppart, ppartner, pmid, psend, precv, load_sems, send_sems, recv_sems):
     rows, width = q_ref.shape
     nh, nz = nd // 4, ns // 2
     chips = nh * nz
@@ -54,15 +53,21 @@
         there = ((h + dh) % nh) * 4 + ((x + dx) % 2) * 2 + (core + dc) % 2
         return (there, ((s + ds) % nz) * 2 + (l + dl) % 2)
 
+    loads = [pltpu.make_async_copy(src, dst, load_sems.at[i])
+             for i, (src, dst) in enumerate(((q_ref, qin), (p_ref, pin), (t_ref, tall.at[0])))]
+    for load in loads:
+        load.start()
     partner = device(dc=1)
     peers = [device(dx=1), device(dl=1), partner]
     peers += [device(dh=dh) for dh in range(1, nh)] + [device(ds=ds) for ds in range(1, nz)]
     barrier = pltpu.get_barrier_semaphore()
     for peer in peers:
         pl.semaphore_signal(barrier, inc=1, device_id=peer, device_id_type=MESH)
-    qall[pl.ds(0, rows), :] = q_ref[...].astype(jnp.bfloat16)
-    pall[pl.ds(0, rows), :] = p_ref[...].astype(jnp.bfloat16)
-    tall[0] = t_ref[...]
+    loads[0].wait()
+    qall[pl.ds(0, rows), :] = qin[...].astype(jnp.bfloat16)
+    loads[1].wait()
+    pall[pl.ds(0, rows), :] = pin[...].astype(jnp.bfloat16)
+    loads[2].wait()
     pl.semaphore_wait(barrier, len(peers))
 
     copies = Copies(send_sems, recv_sems, partner)
@@ -289,6 +294,8 @@
     bf16, f32 = jnp.bfloat16, jnp.float32
     copies = 16 + 5 * CHUNKS + chips * (3 + 4 * CHUNKS)
     scratch = [
+        ((rows, width), f32),
+        ((rows, width), f32),
         ((4 * rows, width), bf16),
         ((cols, width), bf16),
         ((4, 1, rows), jnp.int32),
@@ -306,19 +313,19 @@
         ((max(1, nz + nh - 2) * rows, width), bf16),
         ((max(1, nz + nh - 2) * rows, width), bf16),
     ]
-    held = sum(math.prod(shape) * jnp.dtype(kind).itemsize for shape, kind in scratch)
     vmem = pl.BlockSpec(memory_space=pltpu.VMEM)
     packed = pl.pallas_call(
         functools.partial(kernel, nd, ns),
         out_shape=jax.ShapeDtypeStruct((2 * rows + 8, width), f32),
-        in_specs=[vmem] * 3,
+        in_specs=[pl.BlockSpec(memory_space=pl.ANY)] * 3,
         out_specs=vmem,
         scratch_shapes=[pltpu.VMEM(*entry) for entry in scratch] + [
+            pltpu.SemaphoreType.DMA((3,)),
             pltpu.SemaphoreType.DMA((copies,)),
             pltpu.SemaphoreType.DMA((copies,)),
         ],
         compiler_params=pltpu.CompilerParams(
-            collective_id=0, has_side_effects=True, vmem_limit_bytes=held + 8 * 1024 * 1024
+            collective_id=0, has_side_effects=True, vmem_limit_bytes=64 * 1024 * 1024 - 65536
         ),
     )(queries, passages, positives.reshape(1, rows))
     losses, query_grads, passage_grads = pl.pallas_call(
@@ -330,7 +337,7 @@
         ),
         in_specs=[vmem],
         out_specs=(vmem,) * 3,
-        compiler_params=pltpu.CompilerParams(vmem_limit_bytes=8 * 1024 * 1024),
+        compiler_params=pltpu.CompilerParams(vmem_limit_bytes=64 * 1024 * 1024 - 65536),
     )(packed)
     return losses.reshape(rows), query_grads, passage_grads
 

time: 40.3 us -> 39.6 us (0.983)
  local copies, waits for them, and re-layouts: 2.55 us -> 0 us
  Pallas kernels: 36.9 us -> 38.8 us
    unnamed x6 -> x0, local copies, waits for them, and re-layouts: 2.55 us -> none
    pallas_call x1, Pallas kernels: 0.83 us -> 1.86 us  [body(): pl.pallas_call(unpack, out_shape=(jax.ShapeDtypeStruct((1, rows), f32), j...]
    pallas_call x1, Pallas kernels: 36.1 us -> 36.9 us  [body(): pl.pallas_call(functools.partial(kernel, nd, ns), out_shape=jax.ShapeDtyp...]
where the time goes in v3:
time: 39.6 us; the launch traced here: 39.4 us
  Pallas kernels  38.8 us (98%)
  between operations  0.64 us (2%)
    pallas_call x1, Pallas kernels, body(): pl.pallas_call(functools.partial(kernel, nd, ns), out_shape=jax.ShapeDtyp...  36.9 us
    pallas_call x1, Pallas kernels, body(): pl.pallas_call(unpack, out_shape=(jax.ShapeDtypeStruct((1, rows), f32), j...  1.86 us

profile of v3, /device:TPU:0, one launch (start us, length us, event | category | flops | bytes accessed | tf_op | source)
XLA Modules:
  0.0 39.4 jit_solution(7444157748365675644)
XLA Ops:
  0.6 36.9 %shard_map.58.packed_ref = f32[136,1024]{1,0:T(8,128)} custom-call(f32[64,1024]{1,0:T(8,128)} %q_ref.1, f32[64,1024]{1,0:T(8,128)} %p_ref.1, s32[1,64]{1,0:T(1,128)} %bitcast.2), custom_call_target="tpu_custom_call" | custom-call | tf_op jit(solution)/shard_map/pallas_call | solution.py:317
  37.6 1.9 %shard_map.59 = (f32[1,64]{1,0:T(1,128)}, f32[64,1024]{1,0:T(8,128)}, f32[64,1024]{1,0:T(8,128)}) custom-call(f32[136,1024]{1,0:T(8,128)} %shard_map.58.packed_ref), custom_call_target="tpu_custom_call" | custom-call | tf_op jit(solution)/shard_map/pallas_call | solution.py:331
